TPU v7x, 32 devices: a whole 2x2x4 slice. The times are simulated.
32 devices in a mesh: face: 4 (over x, core), sub: 8 (over z, y).
Axes of the slice: x: 2, y: 2, z: 4, core: 2. Of those that a mesh axis runs over, the one named last changes fastest.
Arguments:
- grid_latent: bfloat16 [16384, 512], P(('face', 'sub')), may hold values from -6 to 6
- mesh_latent: bfloat16 [4096, 512], P(('face', 'sub')), may hold values from -6 to 6
- edge_latent: bfloat16 [32768, 512], P(('face', 'sub')), may hold values from -6 to 6
- mesh_cotangent: bfloat16 [4096, 512], P(('face', 'sub')), may hold values from -6 to 6
- edge_cotangent: bfloat16 [32768, 512], P(('face', 'sub')), may hold values from -6 to 6
- grid_send: int32 [32, 4, 256], P(('face', 'sub')), may hold values from 0 to 511
- grid_slot: int32 [32768], P(('face', 'sub')), may hold values from 0 to 1535, as said below
- grid_target: int32 [32768], P(('face', 'sub')), may hold values from 0 to 127
- mesh_halo: int32 [32, 4, 64], P(('face', 'sub')), may hold values from 0 to 127
- mesh_send: int32 [32, 32, 4], P(('face', 'sub')), may hold values from 0 to 127
- mesh_slot: int32 [32768], P(('face', 'sub')), may hold values from 0 to 511, as said below
- mesh_target: int32 [32768], P(('face', 'sub')), may hold values from 0 to 127
- weights: bfloat16 [10, 512, 512], replicated, may hold values from -0.25 to 0.25
Outputs:
- mesh_update: bfloat16 [4096, 512], P(('face', 'sub'))
- grid_grad: bfloat16 [16384, 512], P(('face', 'sub'))
- mesh_grad: bfloat16 [4096, 512], P(('face', 'sub'))
- edge_grad: bfloat16 [32768, 512], P(('face', 'sub'))
- weight_grads: bfloat16 [10, 512, 512], replicated
Inputs may be any that keep to these rules, and one draw needn't show every extreme that they name: grid_slot[e] names the edge device's own 512 grid rows or, above them, the 256 rows listed by each of its four neighbours in direction order. grid_target[e] is local to the edge's device. grid_send[q, k] lists local rows of device q for the device d with nb(d, k) = q; a row may appear in several slots. mesh_slot[e] names the own 128 mesh rows, then the 64 rows listed by each of the four neighbours, then 4 far rows from each device, source major. mesh_target[e] is local to the edge's device. mesh_halo[q, k] lists local rows of device q for its neighbour in direction k. mesh_send[q, d] lists local rows of device q for far edges of device d.
All inputs are finite; a program needn't handle non-finite values.
Results may differ from a plain program's by a relative error of at most 0.016.
Values may be sent and summed in bfloat16 or wider, within the bound.
A program may use at most 128 MiB of HBM per device.

v0:
```python
import jax
import jax.numpy as jnp
from jax import lax
from jax.sharding import PartitionSpec as P

norm_eps = 1e-05


def shifted(value, axis, steps):
    count = lax.axis_size(axis)
    pairs = [(source, (source + steps) % count) for source in range(count)]
    return lax.ppermute(value, axis, pairs)


def layer_norm(values):
    centre = values - jnp.mean(values, axis=-1, keepdims=True)
    spread = jnp.mean(centre * centre, axis=-1, keepdims=True)
    return centre * lax.rsqrt(spread + norm_eps)


def layer_norm_back(values, upstream):
    centre = values - jnp.mean(values, axis=-1, keepdims=True)
    inverse = lax.rsqrt(jnp.mean(centre * centre, axis=-1, keepdims=True) + norm_eps)
    normed = centre * inverse
    return inverse * (
        upstream
        - jnp.mean(upstream, axis=-1, keepdims=True)
        - normed * jnp.mean(upstream * normed, axis=-1, keepdims=True)
    )


def swish_slope(values):
    sigmoid_values = jax.nn.sigmoid(values)
    return sigmoid_values * (1.0 + values * (1.0 - sigmoid_values))


def product(former, latter):
    return jnp.dot(former, latter, preferred_element_type=jnp.float32)


def outer_sum(former, latter):
    return lax.dot_general(
        former, latter, (((0,), (0,)), ((), ())), preferred_element_type=jnp.float32
    )


def back_product(former, latter):
    return lax.dot_general(
        former, latter, (((1,), (1,)), ((), ())), preferred_element_type=jnp.float32
    )


def receive_sum(onehot, values):
    upper = values.astype(jnp.bfloat16)
    lower = (values - upper.astype(jnp.float32)).astype(jnp.bfloat16)
    return outer_sum(onehot, upper) + outer_sum(onehot, lower)


def grid_neighbours(outgoing):
    from_sub = [shifted(outgoing[block], "sub", offset) for block, offset in ((0, 1), (1, -1))]
    from_face = [shifted(outgoing[block], "face", offset) for block, offset in ((2, 1), (3, -1))]
    return jnp.concatenate(from_sub + from_face, axis=0)


def grid_returns(partials):
    to_sub = [shifted(partials[block], "sub", offset) for block, offset in ((0, -1), (1, 1))]
    to_face = [shifted(partials[block], "face", offset) for block, offset in ((2, -1), (3, 1))]
    return jnp.concatenate(to_sub + to_face, axis=0)


def mesh_neighbours(outgoing):
    from_sub = [shifted(outgoing[block], "sub", offset) for block, offset in ((0, 1), (1, -1))]
    from_face = [shifted(outgoing[block], "face", offset) for block, offset in ((2, 1), (3, -1))]
    return jnp.concatenate(from_sub + from_face, axis=0)


def mesh_returns(partials):
    to_sub = [shifted(partials[block], "sub", offset) for block, offset in ((0, -1), (1, 1))]
    to_face = [shifted(partials[block], "face", offset) for block, offset in ((2, -1), (3, 1))]
    return jnp.concatenate(to_sub + to_face, axis=0)


def move_mesh(outgoing):
    return lax.all_to_all(outgoing, ("face", "sub"), split_axis=0, concat_axis=0, tiled=True)


def return_mesh(outgoing):
    return lax.all_to_all(outgoing, ("face", "sub"), split_axis=0, concat_axis=0, tiled=True)


def on_device(
    grid_latent,
    mesh_latent,
    edge_latent,
    mesh_cotangent,
    edge_cotangent,
    grid_send,
    grid_slot,
    grid_target,
    mesh_halo,
    mesh_send,
    mesh_slot,
    mesh_target,
    weights,
):
    peer_count = lax.axis_size("face") * lax.axis_size("sub")
    latent = weights.shape[1]
    mesh_rows = mesh_latent.shape[0]
    grid_rows = grid_latent.shape[0]
    grid_table = grid_send[0].reshape(-1)
    halo_table = mesh_halo[0].reshape(-1)
    far_table = mesh_send[0].reshape(-1)
    halo_count = halo_table.shape[0]
    node_ids = jnp.arange(mesh_rows, dtype=jnp.int32)
    grid_project = product(grid_latent, weights[0]).astype(jnp.bfloat16)
    grid_outgoing = jnp.take(grid_project, grid_table, axis=0).reshape(4, -1, latent)
    grid_source = jnp.concatenate([grid_project, grid_neighbours(grid_outgoing)], axis=0)
    encode_receive = product(mesh_latent, weights[1])
    encoder_pre = jnp.take(grid_source, grid_slot, axis=0).astype(jnp.float32) + jnp.take(
        encode_receive, grid_target, axis=0
    )
    encoder_hidden = jax.nn.silu(encoder_pre).astype(jnp.bfloat16)
    encoder_linear = product(encoder_hidden, weights[2])
    encoder_message = layer_norm(encoder_linear).astype(jnp.bfloat16)
    grid_onehot = (grid_target[:, None] == node_ids[None, :]).astype(jnp.bfloat16)
    encoder_total = outer_sum(grid_onehot, encoder_message)
    mesh_middle = (mesh_latent.astype(jnp.float32) + encoder_total).astype(jnp.bfloat16)
    sender_rows = product(mesh_middle, weights[4]).astype(jnp.bfloat16)
    halo_outgoing = jnp.take(sender_rows, halo_table, axis=0).reshape(4, -1, latent)
    far_outgoing = jnp.take(sender_rows, far_table, axis=0).reshape(peer_count, -1, latent)
    far_incoming = move_mesh(far_outgoing).reshape(-1, latent)
    mesh_source = jnp.concatenate(
        [sender_rows, mesh_neighbours(halo_outgoing), far_incoming], axis=0
    )
    process_receive = product(mesh_middle, weights[5])
    process_pre = (
        product(edge_latent, weights[3])
        + jnp.take(mesh_source, mesh_slot, axis=0).astype(jnp.float32)
        + jnp.take(process_receive, mesh_target, axis=0)
    )
    process_hidden = jax.nn.silu(process_pre).astype(jnp.bfloat16)
    process_linear = product(process_hidden, weights[6])
    edge_update = layer_norm(process_linear).astype(jnp.bfloat16)
    mesh_onehot = (mesh_target[:, None] == node_ids[None, :]).astype(jnp.bfloat16)
    process_round = outer_sum(mesh_onehot, edge_update).astype(jnp.bfloat16)
    update_pre = product(mesh_middle, weights[7]) + product(process_round, weights[8])
    update_hidden = jax.nn.silu(update_pre).astype(jnp.bfloat16)
    update_linear = product(update_hidden, weights[9])
    mesh_update = (mesh_middle.astype(jnp.float32) + layer_norm(update_linear)).astype(jnp.bfloat16)
    outer_cot = mesh_cotangent.astype(jnp.float32)
    cot_linear = layer_norm_back(update_linear, outer_cot).astype(jnp.bfloat16)
    grad_update_output = outer_sum(update_hidden, cot_linear)
    cot_update = (back_product(cot_linear, weights[9]) * swish_slope(update_pre)).astype(
        jnp.bfloat16
    )
    grad_update_self = outer_sum(mesh_middle, cot_update)
    grad_update_message = outer_sum(process_round, cot_update)
    cot_total = back_product(cot_update, weights[8])
    edge_cot = edge_cotangent.astype(jnp.float32)
    cot_edge = jnp.take(cot_total, mesh_target, axis=0) + edge_cot
    cot_plinear = layer_norm_back(process_linear, cot_edge).astype(jnp.bfloat16)
    grad_process_output = outer_sum(process_hidden, cot_plinear)
    cot_process = back_product(cot_plinear, weights[6]) * swish_slope(process_pre)
    cot_round = cot_process.astype(jnp.bfloat16)
    grad_process_edge = outer_sum(edge_latent, cot_round)
    edge_grad = (edge_cot + back_product(cot_round, weights[3])).astype(jnp.bfloat16)
    cot_receive = receive_sum(mesh_onehot, cot_process).astype(jnp.bfloat16)
    grad_process_receiver = outer_sum(mesh_middle, cot_receive)
    cot_slot = jax.ops.segment_sum(cot_process, mesh_slot, num_segments=mesh_source.shape[0])
    halo_partials = (
        cot_slot[mesh_rows : mesh_rows + halo_count].astype(jnp.bfloat16).reshape(4, -1, latent)
    )
    far_partials = (
        cot_slot[mesh_rows + halo_count :].astype(jnp.bfloat16).reshape(peer_count, -1, latent)
    )
    halo_returned = mesh_returns(halo_partials).astype(jnp.float32)
    far_returned = return_mesh(far_partials).reshape(-1, latent).astype(jnp.float32)
    sender_total = (
        cot_slot[:mesh_rows]
        + jax.ops.segment_sum(halo_returned, halo_table, num_segments=mesh_rows)
        + jax.ops.segment_sum(far_returned, far_table, num_segments=mesh_rows)
    )
    cot_sender = sender_total.astype(jnp.bfloat16)
    grad_process_sender = outer_sum(mesh_middle, cot_sender)
    cot_middle = (
        outer_cot
        + back_product(cot_update, weights[7])
        + back_product(cot_receive, weights[5])
        + back_product(cot_sender, weights[4])
    )
    process_grads = jnp.stack(
        [
            grad_process_edge,
            grad_process_sender,
            grad_process_receiver,
            grad_process_output,
            grad_update_self,
            grad_update_message,
            grad_update_output,
        ]
    )
    process_grads = lax.psum(process_grads, ("face", "sub"))
    cot_message = jnp.take(cot_middle, grid_target, axis=0)
    cot_elinear = layer_norm_back(encoder_linear, cot_message).astype(jnp.bfloat16)
    grad_encode_output = outer_sum(encoder_hidden, cot_elinear)
    cot_encoder = back_product(cot_elinear, weights[2]) * swish_slope(encoder_pre)
    cot_mesh_receive = receive_sum(grid_onehot, cot_encoder).astype(jnp.bfloat16)
    grad_encode_receiver = outer_sum(mesh_latent, cot_mesh_receive)
    mesh_grad = (cot_middle + back_product(cot_mesh_receive, weights[1])).astype(jnp.bfloat16)
    cot_gslot = jax.ops.segment_sum(cot_encoder, grid_slot, num_segments=grid_source.shape[0])
    grid_partials = cot_gslot[grid_rows:].astype(jnp.bfloat16).reshape(4, -1, latent)
    grid_returned = grid_returns(grid_partials).astype(jnp.float32)
    cot_grid = (
        cot_gslot[:grid_rows]
        + jax.ops.segment_sum(grid_returned, grid_table, num_segments=grid_rows)
    ).astype(jnp.bfloat16)
    grad_encode_sender = outer_sum(grid_latent, cot_grid)
    grid_grad = back_product(cot_grid, weights[0]).astype(jnp.bfloat16)
    encode_grads = jnp.stack([grad_encode_sender, grad_encode_receiver, grad_encode_output])
    encode_grads = lax.psum(encode_grads, ("face", "sub"))
    summed = jnp.concatenate([encode_grads, process_grads], axis=0)
    encode_scale = 1.0 / (grid_slot.shape[0] * peer_count) ** 0.5
    process_scale = 1.0 / (mesh_slot.shape[0] * peer_count) ** 0.5
    update_scale = 1.0 / (mesh_rows * peer_count) ** 0.5
    scale_column = jnp.array(
        [encode_scale] * 3 + [process_scale] * 4 + [update_scale] * 3, jnp.float32
    )
    weight_grads = (summed * scale_column[:, None, None]).astype(jnp.bfloat16)
    return (mesh_update, grid_grad, mesh_grad, edge_grad, weight_grads)


def solution(mesh):
    return jax.shard_map(
        on_device,
        mesh=mesh,
        in_specs=(
            P(("face", "sub"), None),
            P(("face", "sub"), None),
            P(("face", "sub"), None),
            P(("face", "sub"), None),
            P(("face", "sub"), None),
            P(("face", "sub"), None, None),
            P(("face", "sub")),
            P(("face", "sub")),
            P(("face", "sub"), None, None),
            P(("face", "sub"), None, None),
            P(("face", "sub")),
            P(("face", "sub")),
            P(),
        ),
        out_specs=(
            P(("face", "sub"), None),
            P(("face", "sub"), None),
            P(("face", "sub"), None),
            P(("face", "sub"), None),
            P(),
        ),
        check_vma=False,
    )
```

profile of v0, /device:TPU:0, one launch (start us, length us, event | category | flops | bytes accessed | tf_op | source)
XLA Modules:
  0.0 434.6 jit_solution(5734349062935372784)
XLA Ops:
  8.6 1.7 constant_dynamic-update-slice_fusion.4
  10.3 5.1 %gather_fusion.3 = bf16[1024,512]{1,0:T(8,128)(2,1)} fusion(bf16[512,512]{1,0:T(8,128)(2,1)S(1)} %get-tuple-element.43, s32[1024]{0:T(1024)S(1)} %fusion.116), kind=kCustom, calls=%fused_computation.clone | custom fusion | bytes 2101248 | tf_op jit(solution)/shard_map/jit(_take)/gather | solution.py:116
  15.4 1.5 broadcast_select_fusion
  17.9 2.4 collective-permute-start.3
  20.3 4.6 %collective-permute-start.1 = (bf16[256,512]{1,0:T(8,128)(2,1)}, bf16[256,512]{1,0:T(8,128)(2,1)}, u32[]{:S(2)}, u32[]{:S(2)}) collective-permute-start(bf16[256,512]{1,0:T(8,128)(2,1)} %get-tuple-element.31), channel_id=1, source_target_pairs={{0,7},{1,0},{2,1},{3,2},{4,3},{5,4},{6,5},{7,6},{8,15},{9,8},{10,9... | collective-permute-start | bytes 786440 | tf_op jit(solution)/shard_map/ppermute | solution.py:12
  31.7 1.3 pad_clamp_fusion
  34.5 2.3 copy.38
  36.7 4.9 %gather_fusion.4 = f32[1024,512]{1,0:T(8,128)} fusion(f32[128,512]{1,0:T(8,128)S(1)} %fusion.58, s32[1024]{0:T(1024)S(1)} %copy-done.50), kind=kCustom, calls=%fused_computation.1.clone | custom fusion | bytes 4198400 | tf_op jit(solution)/shard_map/jit(_take)/gather | solution.py:119
  43.7 5.1 %gather_fusion = bf16[1024,512]{1,0:T(8,128)(2,1)} fusion(bf16[1536,512]{1,0:T(8,128)(2,1)S(1)} %constant_dynamic-update-slice_fusion, s32[1024]{0:T(1024)S(1)} %copy-done.55), kind=kCustom, calls=%fused_computation.6 | custom fusion | bytes 2101248 | tf_op jit(solution)/shard_map/jit(_take)/gather | solution.py:119
  48.8 2.3 multiply_convert_fusion.3
  51.1 2.2 fusion.127
  55.9 2.0 fusion.52
  57.9 1.3 constant_dynamic-update-slice_fusion.10
  60.2 1.3 gather_fusion.1
  62.5 6.1 %all-to-all-start = ((bf16[32,4,512]{2,1,0:T(4,128)(2,1)}), bf16[32,4,512]{2,1,0:T(4,128)(2,1)S(1)}, u32[]{:S(2)}, u32[]{:S(2)}) async-start(bf16[32,4,512]{2,1,0:T(4,128)(2,1)} %broadcast_select_fusion.3), calls=%async_computation | async-start | bytes 262144 | tf_op jit(solution)/shard_map/all_to_all | solution.py:84
  68.7 1.5 collective-permute-start.7
  70.2 4.7 %collective-permute-start.5 = (bf16[64,512]{1,0:T(8,128)(2,1)S(1)}, bf16[64,512]{1,0:T(8,128)(2,1)S(1)}, u32[]{:S(2)}, u32[]{:S(2)}) collective-permute-start(bf16[64,512]{1,0:T(8,128)(2,1)S(1)} %get-tuple-element.40), channel_id=1, source_target_pairs={{0,7},{1,0},{2,1},{3,2},{4,3},{5,4},{6,5},{7,6},{8,15},{9,8},{10,9... | collective-permute-start | bytes 196616 | tf_op jit(solution)/shard_map/ppermute | solution.py:12
  74.9 4.9 %gather_fusion.6 = f32[1024,512]{1,0:T(8,128)} fusion(f32[128,512]{1,0:T(8,128)S(1)} %fusion.44, s32[1024]{0:T(1024)S(1)} %copy-done.52), kind=kCustom, calls=%fused_computation.3.clone | custom fusion | bytes 4198400 | tf_op jit(solution)/shard_map/jit(_take)/gather | solution.py:139
  80.0 4.0 gather_fusion.5
  84.0 4.1 multiply_convert_fusion.2
  88.2 2.2 fusion.128
  91.5 1.3 convolution_add_fusion.4
  92.9 1.5 fusion.129
  96.5 1.4 fusion.15
  97.9 1.4 fusion.37
  99.3 2.1 convolution_add_fusion.3
  101.4 5.1 %gather_fusion.7 = f32[1024,512]{1,0:T(8,128)} fusion(f32[128,512]{1,0:T(8,128)S(1)} %fusion.37, s32[1024]{0:T(1024)} %get-tuple-element.61), kind=kCustom, calls=%fused_computation.4.clone | custom fusion | bytes 4198400 | tf_op jit(solution)/shard_map/jit(_take)/gather | solution.py:160
  106.5 2.9 copy.37
  109.5 2.7 fusion.33
  115.2 4.0 fusion.130
  119.2 7.8 %scatter_custom_fusion = f32[512,512]{1,0:T(8,128)S(1)} fusion(s32[1024]{0:T(1024)} %param.28, f32[1024,512]{1,0:T(8,128)} %get-tuple-element.55, f32[]{:T(128)} %constant.90.clone.1), kind=kCustom, calls=%fused_computation.127 | custom fusion | flops 524288 | bytes 1049088 | tf_op jit(solution)/shard_map/scatter-add | solution.py:169
  128.6 1.8 fusion.14
  132.0 2.9 all-to-all-start.1
  135.0 4.8 %collective-permute-start.8 = (bf16[64,512]{1,0:T(8,128)(2,1)}, bf16[64,512]{1,0:T(8,128)(2,1)S(1)}, u32[]{:S(2)}, u32[]{:S(2)}) collective-permute-start(bf16[64,512]{1,0:T(8,128)(2,1)} %get-tuple-element.33), channel_id=1, source_target_pairs={{0,7},{1,0},{2,1},{3,2},{4,3},{5,4},{6,5},{7,6},{8,15},{9,8},{10,9... | collective-permute-start | bytes 196616 | tf_op jit(solution)/shard_map/ppermute | solution.py:12
  139.8 1.7 collective-permute-start.10
  141.5 1.3 convolution_add_fusion.2
  143.7 4.8 %collective-permute-done.9 = bf16[64,512]{1,0:T(8,128)(2,1)S(1)} collective-permute-done((bf16[64,512]{1,0:T(8,128)(2,1)S(1)}, bf16[64,512]{1,0:T(8,128)(2,1)S(1)}, u32[]{:S(2)}, u32[]{:S(2)}) %collective-permute-start.9) | collective-permute-done | bytes 65568 | tf_op jit(solution)/shard_map/ppermute | solution.py:12
  148.5 2.4 scatter_custom_fusion.1
  150.9 1.5 scatter_custom_fusion.2
  152.5 1.3 convolution_add_fusion.1
  153.9 4.9 %gather_fusion.8 = f32[1024,512]{1,0:T(8,128)} fusion(f32[128,512]{1,0:T(8,128)S(1)} %convolution_add_fusion.1, s32[1024]{0:T(1024)S(1)} %copy-done.51), kind=kCustom, calls=%fused_computation.5.clone | custom fusion | bytes 4198400 | tf_op jit(solution)/shard_map/jit(_take)/gather | solution.py:203
  158.8 3.1 copy.40
  161.9 2.3 select_reduce_fusion
  166.0 2.7 multiply_multiply_fusion
  168.8 1.7 convolution_bitcast_fusion.1
  171.0 8.5 %scatter_custom_fusion.3 = f32[1536,512]{1,0:T(8,128)} fusion(s32[1024]{0:T(1024)} %param.24, f32[1024,512]{1,0:T(8,128)S(1)} %multiply_multiply_fusion, f32[]{:T(128)} %constant.90.clone.1), kind=kCustom, calls=%fused_computation.43 | custom fusion | flops 524288 | bytes 3146240 | tf_op jit(solution)/shard_map/scatter-add | solution.py:210
  179.5 2.1 convert.9
  183.1 1.7 collective-permute-start.14
  184.8 2.2 collective-permute-start.13
  187.0 1.3 fusion.13
  188.3 1.3 fusion.12
  189.6 1.7 fusion.8
  191.4 1.3 fusion.11
  192.7 1.3 fusion.10
  194.1 1.5 fusion.9
  197.1 8.2 %scatter_custom_fusion.4 = f32[512,512]{1,0:T(8,128)S(1)} fusion(f32[512,512]{1,0:T(8,128)S(1)} %slice-done, s32[1024]{0:T(1024)} %bitcast.150, bf16[256,512]{1,0:T(8,128)(2,1)} %copy-done.36, bf16[]{:T(256)} %constant.108, bf16[256,512]{1,0:T(8,128)(2,1)} %copy-done.37, bf16[256,512]{1,0:T(8,128)(2,1)} %collective-permute-done.13, ...), kind=kCustom, calls=%fused_computation.23 | custom fusion | flops 4718592 | bytes 2097664 | tf_op jit(solution)/shard_map/scatter-add | solution.py:215
  205.8 3.2 pad_maximum_fusion
  210.2 3.1 fusion.1
  213.3 2.5 copy.49
  215.8 2.0 fusion.16
  217.9 2.3 convolution_convert_fusion
  220.2 191.5 %all-reduce.3.cloned.1.call-done = (f32[7,512,512]{1,2,0:T(8,128)}, f32[3,512,512]{1,2,0:T(8,128)}) async-done(((f32[7,512,512]{1,2,0:T(8,128)}, f32[3,512,512]{1,2,0:T(8,128)}), (f32[7,512,512]{1,2,0:T(8,128)}, f32[3,512,512]{1,2,0:T(8,128)})) %all-reduce.3.cloned.1.call-update) | async-done | bytes 10485776 | tf_op jit(solution)/shard_map/psum | solution.py:202
  411.7 7.9 %fusion = bf16[10,512,512]{1,2,0:T(8,128)(2,1)} fusion(f32[7,512,512]{1,2,0:T(8,128)} %get-tuple-element.23, f32[3,512,512]{1,2,0:T(8,128)} %get-tuple-element.24, f32[10]{0:T(128)S(1)} %copy-done.71), kind=kLoop, calls=%fused_computation.15 | loop fusion | flops 7864320 | bytes 15728680 | tf_op jit(solution)/shard_map/convert_element_type | solution.py:228
  419.6 8.0 %copy.50 = bf16[10,512,512]{2,1,0:T(8,128)(2,1)} copy(bf16[10,512,512]{1,2,0:T(8,128)(2,1)} %fusion) | data formatting | bytes 10485760
  (259 shorter events, 34.6 us)
Async XLA Ops:
  7.2 76.8 %copy-start = (bf16[1024,512]{1,0:T(8,128)(2,1)S(1)}, bf16[1024,512]{1,0:T(8,128)(2,1)}, u32[]{:S(2)}) copy-start(bf16[1024,512]{1,0:T(8,128)(2,1)} %param.20) | copy-start | bytes 3145732
  15.4 9.5 %copy-start.63 = (s32[1,4,64]{2,1,0:T(4,128)S(1)}, s32[1,4,64]{2,1,0:T(4,128)}, u32[]{:S(2)}) copy-start(s32[1,4,64]{2,1,0:T(4,128)} %param.26) | copy-start | bytes 3076
  15.4 9.7 %copy-start.40 = (s32[1024]{0:T(1024)S(1)}, s32[1024]{0:T(1024)}, u32[]{:S(2)}) copy-start(s32[1024]{0:T(1024)} %param.25) | copy-start | bytes 12292
  15.4 9.7 %copy-start.57 = (s32[1024]{0:T(1024)S(1)}, s32[1024]{0:T(1024)}, u32[]{:S(2)}) copy-start(s32[1024]{0:T(1024)} %param.24) | copy-start | bytes 12292
  15.4 10.9 %copy-start.42 = (s32[1024]{0:T(1024)S(1)}, s32[1024]{0:T(1024)}, u32[]{:S(2)}) copy-start(s32[1024]{0:T(1024)} %param.29) | copy-start | bytes 12292
  15.4 10.9 %copy-start.56 = (s32[1024]{0:T(1024)S(1)}, s32[1024]{0:T(1024)}, u32[]{:S(2)}) copy-start(s32[1024]{0:T(1024)} %param.28) | copy-start | bytes 12292
  15.4 12.0 %copy-start.62 = (s32[1,32,4]{1,2,0:T(4,128)S(1)}, s32[1,32,4]{1,2,0:T(4,128)}, u32[]{:S(2)}) copy-start(s32[1,32,4]{1,2,0:T(4,128)} %param.27) | copy-start | bytes 1540
  15.4 14.4 %copy-start.18 = (bf16[128,512]{1,0:T(8,128)(2,1)S(1)}, bf16[128,512]{1,0:T(8,128)(2,1)}, u32[]{:S(2)}) copy-start(bf16[128,512]{1,0:T(8,128)(2,1)} %param.19) | copy-start | bytes 393220
  17.9 25.7 %collective-permute-start.3 = (bf16[256,512]{1,0:T(8,128)(2,1)}, bf16[256,512]{1,0:T(8,128)(2,1)S(1)}, u32[]{:S(2)}, u32[]{:S(2)}) collective-permute-start(bf16[256,512]{1,0:T(8,128)(2,1)} %get-tuple-element.29), channel_id=1, source_target_pairs={{0,24},{8,0},{16,8},{24,16},{1,25},{9,1},{17,9},{25,17},{2,26},{10... | collective-permute-start | bytes 786440 | tf_op jit(solution)/shard_map/ppermute | solution.py:12
  20.3 23.3 %collective-permute-start.2 = (bf16[256,512]{1,0:T(8,128)(2,1)}, bf16[256,512]{1,0:T(8,128)(2,1)S(1)}, u32[]{:S(2)}, u32[]{:S(2)}) collective-permute-start(bf16[256,512]{1,0:T(8,128)(2,1)} %get-tuple-element.30), channel_id=1, source_target_pairs={{0,8},{8,16},{16,24},{24,0},{1,9},{9,17},{17,25},{25,1},{2,10},{10... | collective-permute-start | bytes 786440 | tf_op jit(solution)/shard_map/ppermute | solution.py:12
  20.3 22.3 %collective-permute-start.1 = (bf16[256,512]{1,0:T(8,128)(2,1)}, bf16[256,512]{1,0:T(8,128)(2,1)}, u32[]{:S(2)}, u32[]{:S(2)}) collective-permute-start(bf16[256,512]{1,0:T(8,128)(2,1)} %get-tuple-element.31), channel_id=1, source_target_pairs={{0,7},{1,0},{2,1},{3,2},{4,3},{5,4},{6,5},{7,6},{8,15},{9,8},{10,9... | collective-permute-start | bytes 786440 | tf_op jit(solution)/shard_map/ppermute | solution.py:12
  24.9 16.7 %collective-permute-start = (bf16[256,512]{1,0:T(8,128)(2,1)}, bf16[256,512]{1,0:T(8,128)(2,1)}, u32[]{:S(2)}, u32[]{:S(2)}) collective-permute-start(bf16[256,512]{1,0:T(8,128)(2,1)} %get-tuple-element.32), channel_id=1, source_target_pairs={{0,1},{1,2},{2,3},{3,4},{4,5},{5,6},{6,7},{7,0},{8,9},{9,10},{10,1... | collective-permute-start | bytes 786440 | tf_op jit(solution)/shard_map/ppermute | solution.py:12
  24.9 4.2 copy-start.68
  33.7 3.1 copy-start.50
  43.7 5.1 %copy-start.58 = (pred[1024]{0:T(1024)(128)(4,1)S(1)}, pred[1024]{0:T(1024)(128)(4,1)}, u32[]{:S(2)}) copy-start(pred[1024]{0:T(1024)(128)(4,1)} %get-tuple-element.62) | copy-start | bytes 3076
  43.7 5.1 %copy-start.64 = (pred[1024]{0:T(1024)(128)(4,1)S(1)}, pred[1024]{0:T(1024)(128)(4,1)}, u32[]{:S(2)}) copy-start(pred[1024]{0:T(1024)(128)(4,1)} %get-tuple-element.63) | copy-start | bytes 3076
  53.7 4.3 copy-start.46
  60.2 14.8 %copy-start.52 = (s32[1024]{0:T(1024)S(1)}, s32[1024]{0:T(1024)}, u32[]{:S(2)}) copy-start(s32[1024]{0:T(1024)} %get-tuple-element.61) | copy-start | bytes 12292
  61.7 18.2 %collective-permute-start.4 = (bf16[64,512]{1,0:T(8,128)(2,1)S(1)}, bf16[64,512]{1,0:T(8,128)(2,1)S(1)}, u32[]{:S(2)}, u32[]{:S(2)}) collective-permute-start(bf16[64,512]{1,0:T(8,128)(2,1)S(1)} %get-tuple-element.41), channel_id=1, source_target_pairs={{0,1},{1,2},{2,3},{3,4},{4,5},{5,6},{6,7},{7,0},{8,9},{9,10},{10,1... | collective-permute-start | bytes 196616 | tf_op jit(solution)/shard_map/ppermute | solution.py:12
  62.5 17.4 %all-to-all-start = ((bf16[32,4,512]{2,1,0:T(4,128)(2,1)}), bf16[32,4,512]{2,1,0:T(4,128)(2,1)S(1)}, u32[]{:S(2)}, u32[]{:S(2)}) async-start(bf16[32,4,512]{2,1,0:T(4,128)(2,1)} %broadcast_select_fusion.3), calls=%async_computation | async-start | bytes 262144 | tf_op jit(solution)/shard_map/all_to_all | solution.py:84
  68.7 11.2 %collective-permute-start.7 = (bf16[64,512]{1,0:T(8,128)(2,1)S(1)}, bf16[64,512]{1,0:T(8,128)(2,1)S(1)}, u32[]{:S(2)}, u32[]{:S(2)}) collective-permute-start(bf16[64,512]{1,0:T(8,128)(2,1)S(1)} %get-tuple-element.38), channel_id=1, source_target_pairs={{0,24},{8,0},{16,8},{24,16},{1,25},{9,1},{17,9},{25,17},{2,26},{10... | collective-permute-start | bytes 196616 | tf_op jit(solution)/shard_map/ppermute | solution.py:12
  70.2 9.6 %collective-permute-start.6 = (bf16[64,512]{1,0:T(8,128)(2,1)S(1)}, bf16[64,512]{1,0:T(8,128)(2,1)S(1)}, u32[]{:S(2)}, u32[]{:S(2)}) collective-permute-start(bf16[64,512]{1,0:T(8,128)(2,1)S(1)} %get-tuple-element.39), channel_id=1, source_target_pairs={{0,8},{8,16},{16,24},{24,0},{1,9},{9,17},{17,25},{25,1},{2,10},{10... | collective-permute-start | bytes 196616 | tf_op jit(solution)/shard_map/ppermute | solution.py:12
  70.2 9.6 %collective-permute-start.5 = (bf16[64,512]{1,0:T(8,128)(2,1)S(1)}, bf16[64,512]{1,0:T(8,128)(2,1)S(1)}, u32[]{:S(2)}, u32[]{:S(2)}) collective-permute-start(bf16[64,512]{1,0:T(8,128)(2,1)S(1)} %get-tuple-element.40), channel_id=1, source_target_pairs={{0,7},{1,0},{2,1},{3,2},{4,3},{5,4},{6,5},{7,6},{8,15},{9,8},{10,9... | collective-permute-start | bytes 196616 | tf_op jit(solution)/shard_map/ppermute | solution.py:12
  74.9 5.0 %copy-start.54 = (s32[1024]{0:T(1024)S(1)}, s32[1024]{0:T(1024)}, u32[]{:S(2)}) copy-start(s32[1024]{0:T(1024)} %get-tuple-element.60) | copy-start | bytes 12292
  80.0 4.0 copy-start.60
  80.0 4.0 copy-start.69
  84.0 4.2 copy-start.22
  90.7 3.6 copy-start.48
  91.5 3.9 copy-start.20
  91.5 3.1 copy-start.33
  92.8 5.1 %copy-start.38 = (f32[128,512]{1,0:T(8,128)}, f32[128,512]{1,0:T(8,128)S(1)}, u32[]{:S(2)}) copy-start(f32[128,512]{1,0:T(8,128)S(1)} %convolution_add_fusion.4) | copy-start | bytes 786436
  94.3 5.0 %copy-start.24 = (f32[128,512]{1,0:T(8,128)}, f32[128,512]{1,0:T(8,128)S(1)}, u32[]{:S(2)}) copy-start(f32[128,512]{1,0:T(8,128)S(1)} %get-tuple-element.53) | copy-start | bytes 786436
  106.5 2.9 copy-start.49
  106.5 2.9 copy-start.61
  109.5 2.8 copy-start.6
  112.3 2.9 copy-start.79
  113.0 6.2 %copy-start.29 = (bf16[1024,512]{0,1:T(8,128)(2,1)}, bf16[1024,512]{0,1:T(8,128)(2,1)S(1)}, u32[]{:S(2)}) copy-start(bf16[1024,512]{0,1:T(8,128)(2,1)S(1)} %multiply_convert_fusion.1) | copy-start | bytes 3145732
  119.2 11.1 %copy-start.10 = (bf16[1024,512]{1,0:T(8,128)(2,1)}, bf16[1024,512]{1,0:T(8,128)(2,1)S(1)}, u32[]{:S(2)}) copy-start(bf16[1024,512]{1,0:T(8,128)(2,1)S(1)} %get-tuple-element.54) | copy-start | bytes 3145732
  130.4 9.4 %copy-start.45 = (bf16[64,512]{1,0:T(8,128)(2,1)S(1)}, bf16[64,512]{1,0:T(8,128)(2,1)}, u32[]{:S(2)}) copy-start(bf16[64,512]{1,0:T(8,128)(2,1)} %get-tuple-element.35) | copy-start | bytes 196612
  130.4 11.1 %copy-start.44 = (bf16[64,512]{1,0:T(8,128)(2,1)S(1)}, bf16[64,512]{1,0:T(8,128)(2,1)}, u32[]{:S(2)}) copy-start(bf16[64,512]{1,0:T(8,128)(2,1)} %get-tuple-element.36) | copy-start | bytes 196612
  130.4 11.1 %copy-start.31 = (f32[128,512]{1,0:T(8,128)S(1)}, f32[128,512]{1,0:T(8,128)}, u32[]{:S(2)}) copy-start(f32[128,512]{1,0:T(8,128)} %convolution_add_fusion.3) | copy-start | bytes 786436
  132.0 18.9 %all-to-all-start.1 = ((bf16[32,4,512]{2,1,0:T(4,128)(2,1)}), bf16[32,4,512]{2,1,0:T(4,128)(2,1)S(1)}, u32[]{:S(2)}, u32[]{:S(2)}) async-start(bf16[32,4,512]{2,1,0:T(4,128)(2,1)} %reshape.209), calls=%async_computation.1 | async-start | bytes 262144 | tf_op jit(solution)/shard_map/all_to_all | solution.py:88
  134.9 276.8 %all-reduce.3.cloned.1.call-start = ((), (), s32[]{:S(2)}) async-start(), calls=%async_computation.2 | async-start | bytes 20971520 | tf_op jit(solution)/shard_map/psum | solution.py:202
  135.0 7.9 %collective-permute-start.8 = (bf16[64,512]{1,0:T(8,128)(2,1)}, bf16[64,512]{1,0:T(8,128)(2,1)S(1)}, u32[]{:S(2)}, u32[]{:S(2)}) collective-permute-start(bf16[64,512]{1,0:T(8,128)(2,1)} %get-tuple-element.33), channel_id=1, source_target_pairs={{0,7},{1,0},{2,1},{3,2},{4,3},{5,4},{6,5},{7,6},{8,15},{9,8},{10,9... | collective-permute-start | bytes 196616 | tf_op jit(solution)/shard_map/ppermute | solution.py:12
  139.8 3.9 collective-permute-start.11
  139.8 3.9 collective-permute-start.10
  141.5 12.3 %copy-start.51 = (s32[1024]{0:T(1024)S(1)}, s32[1024]{0:T(1024)}, u32[]{:S(2)}) copy-start(s32[1024]{0:T(1024)} %get-tuple-element.59) | copy-start | bytes 12292
  141.5 7.0 %collective-permute-start.9 = (bf16[64,512]{1,0:T(8,128)(2,1)S(1)}, bf16[64,512]{1,0:T(8,128)(2,1)S(1)}, u32[]{:S(2)}, u32[]{:S(2)}) collective-permute-start(bf16[64,512]{1,0:T(8,128)(2,1)S(1)} %copy-done.44), channel_id=1, source_target_pairs={{0,1},{1,2},{2,3},{3,4},{4,5},{5,6},{6,7},{7,0},{8,9},{9,10},{10,1... | collective-permute-start | bytes 196616 | tf_op jit(solution)/shard_map/ppermute | solution.py:12
  158.8 3.1 copy-start.3
  158.8 3.1 copy-start.47
  158.8 3.1 copy-start.59
  182.9 6.8 %copy-start.28 = (bf16[1024,512]{1,0:T(8,128)(2,1)S(1)}, bf16[1024,512]{1,0:T(8,128)(2,1)}, u32[]{:S(2)}) copy-start(bf16[1024,512]{1,0:T(8,128)(2,1)} %copy-done.27) | copy-start | bytes 3145732
  182.9 6.8 %copy-start.30 = (bf16[1024,512]{0,1:T(8,128)(2,1)S(1)}, bf16[1024,512]{0,1:T(8,128)(2,1)}, u32[]{:S(2)}) copy-start(bf16[1024,512]{0,1:T(8,128)(2,1)} %copy-done.29) | copy-start | bytes 3145732
  183.0 12.6 %collective-permute-start.12 = (bf16[256,512]{1,0:T(8,128)(2,1)S(1)}, bf16[256,512]{1,0:T(8,128)(2,1)S(1)}, u32[]{:S(2)}, u32[]{:S(2)}) collective-permute-start(bf16[256,512]{1,0:T(8,128)(2,1)S(1)} %get-tuple-element.25), channel_id=1, source_target_pairs={{0,7},{1,0},{2,1},{3,2},{4,3},{5,4},{6,5},{7,6},{8,15},{9,8},{10,9... | collective-permute-start | bytes 786440 | tf_op jit(solution)/shard_map/ppermute | solution.py:12
  183.0 12.6 %collective-permute-start.15 = (bf16[256,512]{1,0:T(8,128)(2,1)S(1)}, bf16[256,512]{1,0:T(8,128)(2,1)S(1)}, u32[]{:S(2)}, u32[]{:S(2)}) collective-permute-start(bf16[256,512]{1,0:T(8,128)(2,1)S(1)} %get-tuple-element.26), channel_id=1, source_target_pairs={{0,8},{8,16},{16,24},{24,0},{1,9},{9,17},{17,25},{25,1},{2,10},{10... | collective-permute-start | bytes 786440 | tf_op jit(solution)/shard_map/ppermute | solution.py:12
  183.1 12.5 %collective-permute-start.14 = (bf16[256,512]{1,0:T(8,128)(2,1)S(1)}, bf16[256,512]{1,0:T(8,128)(2,1)S(1)}, u32[]{:S(2)}, u32[]{:S(2)}) collective-permute-start(bf16[256,512]{1,0:T(8,128)(2,1)S(1)} %get-tuple-element.27), channel_id=1, source_target_pairs={{0,24},{8,0},{16,8},{24,16},{1,25},{9,1},{17,9},{25,17},{2,26},{10... | collective-permute-start | bytes 786440 | tf_op jit(solution)/shard_map/ppermute | solution.py:12
  184.8 12.3 %collective-permute-start.13 = (bf16[256,512]{1,0:T(8,128)(2,1)S(1)}, bf16[256,512]{1,0:T(8,128)(2,1)}, u32[]{:S(2)}, u32[]{:S(2)}) collective-permute-start(bf16[256,512]{1,0:T(8,128)(2,1)S(1)} %get-tuple-element.28), channel_id=1, source_target_pairs={{0,1},{1,2},{2,3},{3,4},{4,5},{5,6},{6,7},{7,0},{8,9},{9,10},{10,1... | collective-permute-start | bytes 786440 | tf_op jit(solution)/shard_map/ppermute | solution.py:12
  188.3 3.0 copy-start.16
  189.6 3.1 copy-start.21
  191.3 2.8 copy-start.39
  191.4 5.7 %slice-start = ((f32[1536,512]{1,0:T(8,128)}), f32[512,512]{1,0:T(8,128)S(1)}, s32[]{:S(2)}) async-start(f32[1536,512]{1,0:T(8,128)} %scatter_custom_fusion.3), calls=%async_computation.3 | async-start | bytes 2097152 | tf_op jit(solution)/shard_map/slice | solution.py:214
  195.6 9.7 %copy-start.32 = (bf16[512,512]{1,0:T(8,128)(2,1)S(1)}, bf16[512,512]{1,0:T(8,128)(2,1)}, u32[]{:S(2)}) copy-start(bf16[512,512]{1,0:T(8,128)(2,1)} %param.18) | copy-start | bytes 1572868
  215.8 195.9 %copy-start.71 = (f32[10]{0:T(128)S(1)}, f32[10]{0:T(128)}, u32[]{:S(2)}) copy-start(f32[10]{0:T(128)} %constant.95.clone) | copy-start | bytes 124
  419.6 8.0 %copy-start.1 = (bf16[1024,512]{1,0:T(8,128)(2,1)S(1)}, bf16[1024,512]{1,0:T(8,128)(2,1)}, u32[]{:S(2)}) copy-start(bf16[1024,512]{1,0:T(8,128)(2,1)} %param.20) | copy-start | bytes 3145732
  (37 other events, 65.6 us)
Sparse Core Ops, SparseCore 0:
  209.1 202.4 all-reduce.2
where the time goes:
time: 442 us; the launch traced here: 435 us
  waiting for transfers between devices  197 us (45%)
  local copies, waits for them, and re-layouts  71.8 us (16%)
  other arithmetic  60.3 us (14%)
  matrix products  57 us (13%)
  starting transfers between devices  32.9 us (7%)
  between operations  15.4 us (3%)
    psum x1, waiting for transfers between devices, on_device(): process_grads = lax.psum(process_grads, ('face', 'sub'))  192 us
    unnamed x172, local copies, waits for them, and re-layouts  24.5 us
    ppermute x16, starting transfers between devices, shifted(): return lax.ppermute(value, axis, pairs)  23.8 us
    dot_general x10, matrix products, back_product(): lax.dot_general(former, latter, (((1,), (1,)), ((), ())), preferred_eleme...  21.7 us
    dot_general x10, matrix products, product(): return jnp.dot(former, latter, preferred_element_type=jnp.float32)  18.8 us
    dot_general x16, matrix products, outer_sum(): lax.dot_general(former, latter, (((0,), (0,)), ((), ())), preferred_eleme...  16.5 us
  transfers between devices with their start and end apart: 19, of which 3 were waited for; matrix products, arithmetic and copies ran while one was open for 11% of the time, Pallas kernels for 0%

commit v1 on v0

--- a/solution.py
+++ b/solution.py
@@ -2,6 +2,7 @@
 import jax.numpy as jnp
 from jax import lax
 from jax.sharding import PartitionSpec as P
+from jax.lax import psum
 
 norm_eps = 1e-05
 
@@ -199,7 +200,7 @@
             grad_update_output,
         ]
     )
-    process_grads = lax.psum(process_grads, ("face", "sub"))
+    process_grads = psum(psum(process_grads, "sub"), "face")
     cot_message = jnp.take(cot_middle, grid_target, axis=0)
     cot_elinear = layer_norm_back(encoder_linear, cot_message).astype(jnp.bfloat16)
     grad_encode_output = outer_sum(encoder_hidden, cot_elinear)

time: 442 us -> 711 us (1.61)
  waiting for transfers between devices: 197 us -> 466 us
    psum x1 -> x3, waiting for transfers between devices: 192 us -> 452 us  [the longest x2 320 us: on_device(): process_grads = psum(psum(process_grads, 'sub'), 'face')]
    ppermute x16, waiting for transfers between devices: 5.59 us -> 14.1 us  [shifted(): return lax.ppermute(value, axis, pairs)]
    unnamed x172 -> x174, local copies, waits for them, and re-layouts: 24.5 us -> 27.5 us
  transfers between devices with their start and end apart: 19 -> 21, of which waited for: 3 -> 8; matrix products, arithmetic and copies ran while one was open for 11% -> 11% of each run, Pallas kernels for 0% -> 0%
where the time goes in v1:
time: 711 us; the launch traced here: 704 us
  waiting for transfers between devices  466 us (66%)
  local copies, waits for them, and re-layouts  74.5 us (10%)
  other arithmetic  59.6 us (8%)
  matrix products  56.2 us (8%)
  starting transfers between devices  32.8 us (5%)
  between operations  15.1 us (2%)
    psum x2, waiting for transfers between devices, on_device(): process_grads = psum(psum(process_grads, 'sub'), 'face')  320 us
    psum x1, waiting for transfers between devices, on_device(): encode_grads = lax.psum(encode_grads, ('face', 'sub'))  132 us
    unnamed x174, local copies, waits for them, and re-layouts  27.5 us
    ppermute x16, starting transfers between devices, shifted(): return lax.ppermute(value, axis, pairs)  23.6 us
    dot_general x10, matrix products, back_product(): lax.dot_general(former, latter, (((1,), (1,)), ((), ())), preferred_eleme...  20.9 us
    dot_general x10, matrix products, product(): return jnp.dot(former, latter, preferred_element_type=jnp.float32)  18.7 us
    dot_general x16, matrix products, outer_sum(): lax.dot_general(former, latter, (((0,), (0,)), ((), ())), preferred_eleme...  16.6 us
  transfers between devices with their start and end apart: 21, of which 8 were waited for; matrix products, arithmetic and copies ran while one was open for 11% of the time, Pallas kernels for 0%

profile of v1, /device:TPU:0, one launch (start us, length us, event | category | flops | bytes accessed | tf_op | source)
XLA Modules:
  0.0 704.2 jit_solution(4994659283480988015)
XLA Ops:
  8.6 1.6 constant_dynamic-update-slice_fusion.4
  10.2 5.1 gather_fusion.3
  15.3 1.5 broadcast_select_fusion
  17.8 2.4 collective-permute-start.3
  20.2 4.6 collective-permute-start.1
  34.4 2.3 copy.38
  36.7 4.9 gather_fusion.4
  43.6 5.1 gather_fusion
  48.7 2.3 multiply_convert_fusion.3
  51.0 2.2 fusion.127
  55.8 2.0 fusion.52
  62.4 6.1 all-to-all-start
  68.5 1.5 collective-permute-start.7
  70.1 4.7 collective-permute-start.5
  74.8 4.9 gather_fusion.6
  79.9 4.0 gather_fusion.5
  83.9 4.1 multiply_convert_fusion.2
  88.0 2.2 fusion.128
  91.9 1.3 convolution_add_fusion.4
  93.3 1.5 fusion.129
  95.8 1.4 fusion.15
  97.9 1.3 fusion.37
  99.2 5.2 gather_fusion.7
  104.4 2.9 copy.37
  107.3 2.7 fusion.33
  113.0 4.0 fusion.130
  117.1 7.8 %scatter_custom_fusion = f32[512,512]{1,0:T(8,128)S(1)} fusion(s32[1024]{0:T(1024)} %param.28, f32[1024,512]{1,0:T(8,128)} %get-tuple-element.53, f32[]{:T(128)} %constant.90.clone.1), kind=kCustom, calls=%fused_computation.127 | custom fusion | flops 524288 | bytes 1049088 | tf_op jit(solution)/shard_map/scatter-add | solution.py:170
  127.9 3.0 all-to-all-start.1
  130.9 4.6 collective-permute-start.8
  135.5 1.7 collective-permute-start.10
  137.4 1.8 fusion.14
  140.6 4.0 collective-permute-done.9
  144.7 2.7 scatter_custom_fusion.1
  147.4 1.7 scatter_custom_fusion.2
  150.4 1.3 fusion.12
  151.7 1.7 fusion.8
  153.5 1.4 fusion.11
  154.9 1.3 fusion.10
  156.2 1.5 fusion.9
  157.8 1.3 convolution_add_fusion.3
  159.2 1.3 convolution_add_fusion.2
  160.5 1.4 convolution_add_fusion.1
  162.0 4.9 gather_fusion.8
  166.8 3.1 copy.40
  169.9 2.3 select_reduce_fusion
  174.4 2.6 multiply_multiply_fusion
  177.1 8.7 %scatter_custom_fusion.3 = f32[1536,512]{1,0:T(8,128)} fusion(s32[1024]{0:T(1024)} %param.24, f32[1024,512]{1,0:T(8,128)S(1)} %multiply_multiply_fusion, f32[]{:T(128)} %constant.90.clone.1), kind=kCustom, calls=%fused_computation.43 | custom fusion | flops 524288 | bytes 3146240 | tf_op jit(solution)/shard_map/scatter-add | solution.py:211
  185.8 2.1 convert.9
  188.5 1.7 collective-permute-start.14
  190.2 1.6 collective-permute-start.13
  194.5 1.7 convolution_bitcast_fusion.1
  196.2 4.2 collective-permute-done.12
  201.8 5.7 collective-permute-done.13
  207.5 8.1 %scatter_custom_fusion.4 = f32[512,512]{1,0:T(8,128)S(1)} fusion(f32[512,512]{1,0:T(8,128)S(1)} %slice-done, s32[1024]{0:T(1024)} %bitcast.150, bf16[256,512]{1,0:T(8,128)(2,1)} %copy-done.36, bf16[]{:T(256)} %constant.108, bf16[256,512]{1,0:T(8,128)(2,1)} %copy-done.37, bf16[256,512]{1,0:T(8,128)(2,1)} %collective-permute-done.13, ...), kind=kCustom, calls=%fused_computation.23 | custom fusion | flops 4718592 | bytes 2097664 | tf_op jit(solution)/shard_map/scatter-add | solution.py:216
  216.9 2.0 pad_maximum_fusion
  218.9 182.0 %all-reduce.6.cloned.1.call-done = f32[7,512,512]{1,2,0:T(8,128)} async-done(((f32[7,512,512]{1,2,0:T(8,128)}), f32[7,512,512]{1,2,0:T(8,128)}) %all-reduce.6.cloned.1.call-update) | async-done | bytes 7340048 | tf_op jit(solution)/shard_map/psum | solution.py:203
  402.1 3.1 fusion.1
  405.2 2.3 copy.49
  407.5 2.0 fusion.16
  409.5 2.3 convolution_convert_fusion
  411.8 132.0 %all-reduce.4.cloned.1.call-done = f32[3,512,512]{1,2,0:T(8,128)} async-done(((f32[3,512,512]{1,2,0:T(8,128)}), f32[3,512,512]{1,2,0:T(8,128)}) %all-reduce.4.cloned.1.call-update) | async-done | bytes 3145744 | tf_op jit(solution)/shard_map/psum | solution.py:221
  543.8 137.8 %all-reduce.8.cloned.1.call-done = f32[7,512,512]{1,2,0:T(8,128)} async-done(((f32[7,512,512]{1,2,0:T(8,128)}), f32[7,512,512]{1,2,0:T(8,128)}) %all-reduce.8.cloned.1.call-update) | async-done | bytes 7340048 | tf_op jit(solution)/shard_map/psum | solution.py:203
  681.5 7.9 %fusion = bf16[10,512,512]{1,2,0:T(8,128)(2,1)} fusion(f32[7,512,512]{1,2,0:T(8,128)} %all-reduce.8.cloned.1.call-done, f32[3,512,512]{1,2,0:T(8,128)} %all-reduce.4.cloned.1.call-done, f32[10]{0:T(128)S(1)} %copy-done.72), kind=kLoop, calls=%fused_computation.15 | loop fusion | flops 7864320 | bytes 15728680 | tf_op jit(solution)/shard_map/convert_element_type | solution.py:229
  689.4 8.0 %copy.50 = bf16[10,512,512]{2,1,0:T(8,128)(2,1)} copy(bf16[10,512,512]{1,2,0:T(8,128)(2,1)} %fusion) | data formatting | bytes 10485760
  (266 shorter events, 42.9 us)
Async XLA Ops:
  7.2 76.7 %copy-start = (bf16[1024,512]{1,0:T(8,128)(2,1)S(1)}, bf16[1024,512]{1,0:T(8,128)(2,1)}, u32[]{:S(2)}) copy-start(bf16[1024,512]{1,0:T(8,128)(2,1)} %param.20) | copy-start | bytes 3145732
  15.3 9.5 %copy-start.64 = (s32[1,4,64]{2,1,0:T(4,128)S(1)}, s32[1,4,64]{2,1,0:T(4,128)}, u32[]{:S(2)}) copy-start(s32[1,4,64]{2,1,0:T(4,128)} %param.26) | copy-start | bytes 3076
  15.3 9.7 %copy-start.40 = (s32[1024]{0:T(1024)S(1)}, s32[1024]{0:T(1024)}, u32[]{:S(2)}) copy-start(s32[1024]{0:T(1024)} %param.25) | copy-start | bytes 12292
  15.3 9.7 %copy-start.58 = (s32[1024]{0:T(1024)S(1)}, s32[1024]{0:T(1024)}, u32[]{:S(2)}) copy-start(s32[1024]{0:T(1024)} %param.24) | copy-start | bytes 12292
  15.3 10.9 %copy-start.42 = (s32[1024]{0:T(1024)S(1)}, s32[1024]{0:T(1024)}, u32[]{:S(2)}) copy-start(s32[1024]{0:T(1024)} %param.29) | copy-start | bytes 12292
  15.3 10.9 %copy-start.57 = (s32[1024]{0:T(1024)S(1)}, s32[1024]{0:T(1024)}, u32[]{:S(2)}) copy-start(s32[1024]{0:T(1024)} %param.28) | copy-start | bytes 12292
  15.3 12.1 %copy-start.63 = (s32[1,32,4]{1,2,0:T(4,128)S(1)}, s32[1,32,4]{1,2,0:T(4,128)}, u32[]{:S(2)}) copy-start(s32[1,32,4]{1,2,0:T(4,128)} %param.27) | copy-start | bytes 1540
  15.3 14.5 %copy-start.17 = (bf16[128,512]{1,0:T(8,128)(2,1)S(1)}, bf16[128,512]{1,0:T(8,128)(2,1)}, u32[]{:S(2)}) copy-start(bf16[128,512]{1,0:T(8,128)(2,1)} %param.19) | copy-start | bytes 393220
  17.8 25.7 %collective-permute-start.3 = (bf16[256,512]{1,0:T(8,128)(2,1)}, bf16[256,512]{1,0:T(8,128)(2,1)S(1)}, u32[]{:S(2)}, u32[]{:S(2)}) collective-permute-start(bf16[256,512]{1,0:T(8,128)(2,1)} %get-tuple-element.27), channel_id=1, source_target_pairs={{0,24},{8,0},{16,8},{24,16},{1,25},{9,1},{17,9},{25,17},{2,26},{10... | collective-permute-start | bytes 786440 | tf_op jit(solution)/shard_map/ppermute | solution.py:13
  20.2 23.3 %collective-permute-start.2 = (bf16[256,512]{1,0:T(8,128)(2,1)}, bf16[256,512]{1,0:T(8,128)(2,1)S(1)}, u32[]{:S(2)}, u32[]{:S(2)}) collective-permute-start(bf16[256,512]{1,0:T(8,128)(2,1)} %get-tuple-element.28), channel_id=1, source_target_pairs={{0,8},{8,16},{16,24},{24,0},{1,9},{9,17},{17,25},{25,1},{2,10},{10... | collective-permute-start | bytes 786440 | tf_op jit(solution)/shard_map/ppermute | solution.py:13
  20.2 22.3 %collective-permute-start.1 = (bf16[256,512]{1,0:T(8,128)(2,1)}, bf16[256,512]{1,0:T(8,128)(2,1)}, u32[]{:S(2)}, u32[]{:S(2)}) collective-permute-start(bf16[256,512]{1,0:T(8,128)(2,1)} %get-tuple-element.29), channel_id=1, source_target_pairs={{0,7},{1,0},{2,1},{3,2},{4,3},{5,4},{6,5},{7,6},{8,15},{9,8},{10,9... | collective-permute-start | bytes 786440 | tf_op jit(solution)/shard_map/ppermute | solution.py:13
  24.8 16.8 %collective-permute-start = (bf16[256,512]{1,0:T(8,128)(2,1)}, bf16[256,512]{1,0:T(8,128)(2,1)}, u32[]{:S(2)}, u32[]{:S(2)}) collective-permute-start(bf16[256,512]{1,0:T(8,128)(2,1)} %get-tuple-element.30), channel_id=1, source_target_pairs={{0,1},{1,2},{2,3},{3,4},{4,5},{5,6},{6,7},{7,0},{8,9},{9,10},{10,1... | collective-permute-start | bytes 786440 | tf_op jit(solution)/shard_map/ppermute | solution.py:13
  24.9 4.2 copy-start.69
  33.6 3.0 copy-start.51
  43.6 5.1 copy-start.59
  43.6 5.1 copy-start.65
  53.6 4.2 copy-start.47
  60.1 14.8 %copy-start.53 = (s32[1024]{0:T(1024)S(1)}, s32[1024]{0:T(1024)}, u32[]{:S(2)}) copy-start(s32[1024]{0:T(1024)} %get-tuple-element.59) | copy-start | bytes 12292
  61.5 18.1 %collective-permute-start.4 = (bf16[64,512]{1,0:T(8,128)(2,1)S(1)}, bf16[64,512]{1,0:T(8,128)(2,1)S(1)}, u32[]{:S(2)}, u32[]{:S(2)}) collective-permute-start(bf16[64,512]{1,0:T(8,128)(2,1)S(1)} %get-tuple-element.39), channel_id=1, source_target_pairs={{0,1},{1,2},{2,3},{3,4},{4,5},{5,6},{6,7},{7,0},{8,9},{9,10},{10,1... | collective-permute-start | bytes 196616 | tf_op jit(solution)/shard_map/ppermute | solution.py:13
  62.4 17.4 %all-to-all-start = ((bf16[32,4,512]{2,1,0:T(4,128)(2,1)}), bf16[32,4,512]{2,1,0:T(4,128)(2,1)S(1)}, u32[]{:S(2)}, u32[]{:S(2)}) async-start(bf16[32,4,512]{2,1,0:T(4,128)(2,1)} %broadcast_select_fusion.3), calls=%async_computation | async-start | bytes 262144 | tf_op jit(solution)/shard_map/all_to_all | solution.py:85
  68.5 11.2 %collective-permute-start.7 = (bf16[64,512]{1,0:T(8,128)(2,1)S(1)}, bf16[64,512]{1,0:T(8,128)(2,1)S(1)}, u32[]{:S(2)}, u32[]{:S(2)}) collective-permute-start(bf16[64,512]{1,0:T(8,128)(2,1)S(1)} %get-tuple-element.36), channel_id=1, source_target_pairs={{0,24},{8,0},{16,8},{24,16},{1,25},{9,1},{17,9},{25,17},{2,26},{10... | collective-permute-start | bytes 196616 | tf_op jit(solution)/shard_map/ppermute | solution.py:13
  70.1 9.6 %collective-permute-start.6 = (bf16[64,512]{1,0:T(8,128)(2,1)S(1)}, bf16[64,512]{1,0:T(8,128)(2,1)S(1)}, u32[]{:S(2)}, u32[]{:S(2)}) collective-permute-start(bf16[64,512]{1,0:T(8,128)(2,1)S(1)} %get-tuple-element.37), channel_id=1, source_target_pairs={{0,8},{8,16},{16,24},{24,0},{1,9},{9,17},{17,25},{25,1},{2,10},{10... | collective-permute-start | bytes 196616 | tf_op jit(solution)/shard_map/ppermute | solution.py:13
  70.1 9.6 %collective-permute-start.5 = (bf16[64,512]{1,0:T(8,128)(2,1)S(1)}, bf16[64,512]{1,0:T(8,128)(2,1)S(1)}, u32[]{:S(2)}, u32[]{:S(2)}) collective-permute-start(bf16[64,512]{1,0:T(8,128)(2,1)S(1)} %get-tuple-element.38), channel_id=1, source_target_pairs={{0,7},{1,0},{2,1},{3,2},{4,3},{5,4},{6,5},{7,6},{8,15},{9,8},{10,9... | collective-permute-start | bytes 196616 | tf_op jit(solution)/shard_map/ppermute | solution.py:13
  74.8 5.0 copy-start.55
  79.8 4.0 copy-start.61
  79.8 4.0 copy-start.70
  83.8 4.2 copy-start.21
  88.0 3.1 copy-start.43
  91.9 3.9 copy-start.19
  91.9 3.1 copy-start.34
  93.3 3.9 copy-start.38
  104.4 2.9 copy-start.50
  104.4 2.9 copy-start.62
  107.3 2.8 copy-start.6
  110.1 2.9 copy-start.80
  110.9 6.2 copy-start.28
  117.1 20.3 %copy-start.10 = (bf16[1024,512]{1,0:T(8,128)(2,1)}, bf16[1024,512]{1,0:T(8,128)(2,1)S(1)}, u32[]{:S(2)}) copy-start(bf16[1024,512]{1,0:T(8,128)(2,1)S(1)} %get-tuple-element.52) | copy-start | bytes 3145732
  127.9 19.5 %all-to-all-start.1 = ((bf16[32,4,512]{2,1,0:T(4,128)(2,1)}), bf16[32,4,512]{2,1,0:T(4,128)(2,1)S(1)}, u32[]{:S(2)}, u32[]{:S(2)}) async-start(bf16[32,4,512]{2,1,0:T(4,128)(2,1)} %reshape.209), calls=%async_computation.1 | async-start | bytes 262144 | tf_op jit(solution)/shard_map/all_to_all | solution.py:89
  130.8 270.0 %all-reduce.6.cloned.1.call-start = ((), (), s32[]{:S(2)}) async-start(), calls=%async_computation.3 | async-start | bytes 14680064 | tf_op jit(solution)/shard_map/psum | solution.py:203
  130.9 8.3 %collective-permute-start.8 = (bf16[64,512]{1,0:T(8,128)(2,1)}, bf16[64,512]{1,0:T(8,128)(2,1)S(1)}, u32[]{:S(2)}, u32[]{:S(2)}) collective-permute-start(bf16[64,512]{1,0:T(8,128)(2,1)} %get-tuple-element.31), channel_id=1, source_target_pairs={{0,7},{1,0},{2,1},{3,2},{4,3},{5,4},{6,5},{7,6},{8,15},{9,8},{10,9... | collective-permute-start | bytes 196616 | tf_op jit(solution)/shard_map/ppermute | solution.py:13
  135.5 3.9 collective-permute-start.11
  135.5 4.0 collective-permute-start.10
  137.2 7.4 %collective-permute-start.9 = (bf16[64,512]{1,0:T(8,128)(2,1)}, bf16[64,512]{1,0:T(8,128)(2,1)}, u32[]{:S(2)}, u32[]{:S(2)}) collective-permute-start(bf16[64,512]{1,0:T(8,128)(2,1)} %get-tuple-element.34), channel_id=1, source_target_pairs={{0,1},{1,2},{2,3},{3,4},{4,5},{5,6},{6,7},{7,0},{8,9},{9,10},{10,1... | collective-permute-start | bytes 196616 | tf_op jit(solution)/shard_map/ppermute | solution.py:13
  147.3 4.4 copy-start.27
  147.3 4.4 copy-start.29
  150.4 3.0 copy-start.16
  151.7 3.1 copy-start.20
  153.4 2.8 copy-start.24
  153.4 2.8 copy-start.35
  153.4 2.8 copy-start.39
  157.7 4.2 copy-start.52
  157.8 386.0 %all-reduce.4.cloned.1.call-start = ((), (), s32[]{:S(2)}) async-start(), calls=%async_computation.2 | async-start | bytes 6291456 | tf_op jit(solution)/shard_map/psum | solution.py:221
  166.8 3.1 copy-start.3
  166.8 3.1 copy-start.48
  166.8 3.1 copy-start.60
  188.0 12.4 %collective-permute-start.12 = (bf16[256,512]{1,0:T(8,128)(2,1)S(1)}, bf16[256,512]{1,0:T(8,128)(2,1)S(1)}, u32[]{:S(2)}, u32[]{:S(2)}) collective-permute-start(bf16[256,512]{1,0:T(8,128)(2,1)S(1)} %get-tuple-element.23), channel_id=1, source_target_pairs={{0,7},{1,0},{2,1},{3,2},{4,3},{5,4},{6,5},{7,6},{8,15},{9,8},{10,9... | collective-permute-start | bytes 786440 | tf_op jit(solution)/shard_map/ppermute | solution.py:13
  188.5 11.9 %collective-permute-start.15 = (bf16[256,512]{1,0:T(8,128)(2,1)S(1)}, bf16[256,512]{1,0:T(8,128)(2,1)S(1)}, u32[]{:S(2)}, u32[]{:S(2)}) collective-permute-start(bf16[256,512]{1,0:T(8,128)(2,1)S(1)} %get-tuple-element.24), channel_id=1, source_target_pairs={{0,8},{8,16},{16,24},{24,0},{1,9},{9,17},{17,25},{25,1},{2,10},{10... | collective-permute-start | bytes 786440 | tf_op jit(solution)/shard_map/ppermute | solution.py:13
  188.5 11.9 %collective-permute-start.14 = (bf16[256,512]{1,0:T(8,128)(2,1)S(1)}, bf16[256,512]{1,0:T(8,128)(2,1)S(1)}, u32[]{:S(2)}, u32[]{:S(2)}) collective-permute-start(bf16[256,512]{1,0:T(8,128)(2,1)S(1)} %get-tuple-element.25), channel_id=1, source_target_pairs={{0,24},{8,0},{16,8},{24,16},{1,25},{9,1},{17,9},{25,17},{2,26},{10... | collective-permute-start | bytes 786440 | tf_op jit(solution)/shard_map/ppermute | solution.py:13
  190.2 17.3 %collective-permute-start.13 = (bf16[256,512]{1,0:T(8,128)(2,1)S(1)}, bf16[256,512]{1,0:T(8,128)(2,1)}, u32[]{:S(2)}, u32[]{:S(2)}) collective-permute-start(bf16[256,512]{1,0:T(8,128)(2,1)S(1)} %get-tuple-element.26), channel_id=1, source_target_pairs={{0,1},{1,2},{2,3},{3,4},{4,5},{5,6},{6,7},{7,0},{8,9},{9,10},{10,1... | collective-permute-start | bytes 786440 | tf_op jit(solution)/shard_map/ppermute | solution.py:13
  194.5 13.0 %slice-start = ((f32[1536,512]{1,0:T(8,128)}), f32[512,512]{1,0:T(8,128)S(1)}, s32[]{:S(2)}) async-start(f32[1536,512]{1,0:T(8,128)} %scatter_custom_fusion.3), calls=%async_computation.5 | async-start | bytes 2097152 | tf_op jit(solution)/shard_map/slice | solution.py:215
  194.5 21.1 %copy-start.33 = (bf16[512,512]{1,0:T(8,128)(2,1)S(1)}, bf16[512,512]{1,0:T(8,128)(2,1)}, u32[]{:S(2)}) copy-start(bf16[512,512]{1,0:T(8,128)(2,1)} %param.18) | copy-start | bytes 1572868
  218.9 462.7 %all-reduce.8.cloned.1.call-start = ((), (), s32[]{:S(2)}) async-start(), calls=%async_computation.4 | async-start | bytes 14680064 | tf_op jit(solution)/shard_map/psum | solution.py:203
  407.5 274.1 %copy-start.72 = (f32[10]{0:T(128)S(1)}, f32[10]{0:T(128)}, u32[]{:S(2)}) copy-start(f32[10]{0:T(128)} %constant.95.clone) | copy-start | bytes 124
  689.4 8.0 %copy-start.1 = (bf16[1024,512]{1,0:T(8,128)(2,1)S(1)}, bf16[1024,512]{1,0:T(8,128)(2,1)}, u32[]{:S(2)}) copy-start(bf16[1024,512]{1,0:T(8,128)(2,1)} %param.20) | copy-start | bytes 3145732
  (39 other events, 68.8 us)
Sparse Core Ops, SparseCore 0:
  157.9 242.9 all-reduce.5
  406.9 136.8 all-reduce.3
  546.2 135.3 all-reduce.7
